TPU v7x, 256 devices: a whole 4x4x8 slice. The times are simulated.
256 devices in a mesh: dp: 16 (over x, z_hi, core), expert: 16 (over y, z_lo).
Axes of the slice: x: 4, y: 4, z: 8 (z_hi: 2, z_lo: 4; z = z_hi * 4 + z_lo), core: 2. Of those that a mesh axis runs over, the one named last changes fastest.
Arguments:
- hidden: bfloat16 [16, 2048, 1792], P('expert', 'dp'), may hold values from -6 to 6
- outgrad: bfloat16 [16, 2048, 4096], P('expert', 'dp'), may hold values from -6 to 6
- row_expert: int32 [16, 2048], P('expert', 'dp'), may hold values from 0 to 1
- counts: int32 [16, 16], P('expert', 'dp'), may hold values from 1 to 128, as said below
- learner_map: int32 [256], replicated, may hold values from 0 to 255, as said below
- rollout_map: int32 [256], replicated, may hold values from 0 to 255, as said below
- master: float32 [4096, 28672], P('dp', 'expert'), may hold values from -3 to 3
- moment1: float32 [4096, 28672], P('dp', 'expert'), may hold values from -12 to 12
- moment2: float32 [4096, 28672], P('dp', 'expert'), may hold values from 1 to 1000
Outputs:
- new_master: float32 [4096, 28672], P('dp', 'expert')
- new_moment1: float32 [4096, 28672], P('dp', 'expert')
- new_moment2: float32 [4096, 28672], P('dp', 'expert')
- rollout_weights: bfloat16 [4096, 28672], P('dp', 'expert')
Inputs may be any that keep to these rules, and one draw needn't show every extreme that they name: `counts`: some device has exactly 128 live rows in every draw. `learner_map`: a permutation of the units. `rollout_map`: a permutation of the units; the 16 units at the positions of one learner device lie at positions of 16 different rollout devices, one each.
All inputs are finite; a program needn't handle non-finite values.
Results may differ from a plain program's by a relative error of at most 0.0095.
Values may be sent and summed in bfloat16 or wider, within the bound.
A program may use at most 128 MiB of HBM per device.

v0:
```python
import jax
import jax.numpy as jnp
from jax import lax
from jax.sharding import Mesh
from jax.sharding import PartitionSpec as P

FF = 14336
DP = ("dp_0", "dp_1", "dp_2")
beta_one = 0.9
beta_two = 0.95
learn_rate = 0.01
decay_rate = 0.1
epsilon = 1e-08
step_count = 100.0


def split_up(value, dim, devices):
    before, after = (value.shape[:dim], value.shape[dim + 1 :])
    return jnp.moveaxis(value.reshape(*before, devices, -1, *after), dim, 0)


def joined_along(blocks, dim):
    blocks = jnp.moveaxis(blocks, 0, dim)
    lengths = blocks.shape
    return blocks.reshape(*lengths[:dim], lengths[dim] * lengths[dim + 1], *lengths[dim + 2 :])


def exchange_in_order(blocks, axes, turns):
    inside = blocks.shape[1:]
    out = blocks.reshape(*(lax.axis_size(a) for a in axes), *inside)
    for k in turns:
        out = lax.all_to_all(out, axes[k], k, k, tiled=True)
    return out.reshape(-1, *inside)


def core_and_chips(value, groups, turns, split_dim, concat_dim):
    devices = lax.axis_size(groups[0]) * lax.axis_size(groups[1])
    blocks = split_up(value, split_dim, devices)
    return joined_along(exchange_in_order(blocks, groups, turns), concat_dim)


def on_device(
    hidden, outgrad, row_expert, counts, learner_map, rollout_map, master, moment1, moment2
):
    hidden = hidden[0]
    outgrad = outgrad[0]
    groups = lax.axis_size("expert")
    own_index = lax.axis_index("expert")
    block_width = hidden.shape[1] // groups
    per_expert = FF // block_width
    tok_rows = hidden.shape[0]
    width_share = master.shape[0]
    slot_units = lax.dynamic_slice_in_dim(learner_map, own_index * groups, groups)
    slot_expert = slot_units // per_expert
    live_rows = jnp.arange(tok_rows, dtype=jnp.int32) < counts[0, 0]
    kept = live_rows[:, None] & (row_expert[0][:, None] == slot_expert[None, :])
    kept_cols = jnp.repeat(kept, block_width, axis=1)
    masked = jnp.where(kept_cols, hidden, jnp.zeros((), jnp.bfloat16))
    contract = (((0,), (0,)), ((), ()))
    sliced = core_and_chips(outgrad, (("dp_0", "dp_1"), "dp_2"), (1, 0), 1, 0)
    gradient = lax.dot_general(
        sliced,
        lax.all_gather(masked, DP, axis=0, tiled=True),
        contract,
        preferred_element_type=jnp.float32,
    )
    new_moment1 = beta_one * moment1 + (1.0 - beta_one) * gradient
    new_moment2 = beta_two * moment2 + (1.0 - beta_two) * gradient * gradient
    bias_one = 1.0 - beta_one**step_count
    bias_two = 1.0 - beta_two**step_count
    update = new_moment1 / bias_one / (jnp.sqrt(new_moment2 / bias_two) + epsilon)
    new_master = master - learn_rate * (update + decay_rate * master)
    inverse_roll = jnp.argsort(rollout_map)
    inverse_learn = jnp.argsort(learner_map)
    target = inverse_roll[slot_units] // groups
    send_order = jnp.argsort(target)
    rounded = new_master.astype(jnp.bfloat16).reshape(width_share, groups, block_width)
    outgoing = jnp.take(rounded, send_order, axis=1).reshape(width_share, groups * block_width)
    incoming = lax.all_to_all(outgoing, "expert", split_axis=1, concat_axis=1, tiled=True).reshape(
        width_share, groups, block_width
    )
    wanted = lax.dynamic_slice_in_dim(rollout_map, own_index * groups, groups)
    source = inverse_learn[wanted] // groups
    rollout_weights = jnp.take(incoming, source, axis=1).reshape(width_share, groups * block_width)
    return (new_master, new_moment1, new_moment2, rollout_weights)


def solution(mesh):
    finer = Mesh(
        mesh.devices.reshape(4, 2, 2, mesh.shape["expert"]), ("dp_0", "dp_1", "dp_2", "expert")
    )
    return jax.shard_map(
        on_device,
        mesh=finer,
        in_specs=(
            P("expert", DP, None),
            P("expert", DP, None),
            P("expert", DP),
            P("expert", DP),
            P(),
            P(),
            P(DP, "expert"),
            P(DP, "expert"),
            P(DP, "expert"),
        ),
        out_specs=(P(DP, "expert"), P(DP, "expert"), P(DP, "expert"), P(DP, "expert")),
        check_vma=False,
    )
```

profile of v0, /device:TPU:1, one launch (start us, length us, event | category | flops | bytes accessed | tf_op | source)
XLA Modules:
  0.0 188.4 jit_solution(5097774377998562409)
XLA Ops:
  8.0 1.3 copy.53
  9.2 0.8 compare_select_fusion.3
  10.0 0.7 compare_and_fusion
  10.8 0.8 bitcast_select_fusion
  12.8 7.4 %all_to_all.16 = bf16[8,2,128,256]{3,2,0,1:T(8,128)(2,1)S(1)} all-to-all(bf16[8,2,128,256]{3,2,0,1:T(8,128)(2,1)S(1)} %copy.56), channel_id=1, replica_groups=mesh['dp_0'=4,'dp_1'=2,'dp_2'=2,'expert'=16] {'dp_2'}, dimensions={1} | all-to-all | bytes 2097152 | tf_op jit(solution)/shard_map/all_to_all | solution.py:32
  20.2 1.0 copy.57
  21.3 8.9 %all-to-all-start.1 = ((bf16[8,2,128,256]{3,2,1,0:T(8,128)(2,1)}), bf16[8,2,128,256]{3,2,1,0:T(8,128)(2,1)S(1)}, u32[]{:S(2)}, u32[]{:S(2)}) async-start(bf16[8,2,128,256]{3,2,1,0:T(8,128)(2,1)} %copy.57), calls=%async_computation.1 | async-start | bytes 2097152 | tf_op jit(solution)/shard_map/all_to_all | solution.py:32
  30.2 1.7 copy.52
  31.9 2.9 %copy.58 = f32[256,1792]{0,1:T(8,128)} copy(f32[256,1792]{1,0:T(8,128)} %param.19) | data formatting | bytes 3670016 | tf_op args[8]
  34.7 1.7 copy.60
  36.4 3.1 %sort.48 = (s32[256]{0:T(256)}, s32[256]{0:T(256)S(1)}) sort(s32[256]{0:T(256)S(1)} %copy-done.4, s32[256]{0:T(256)S(1)} %iota.17), dimensions={0}, to_apply=%region_0.1 | sort | flops 2048 | bytes 4096 | tf_op jit(solution)/shard_map/jit(argsort)/sort | solution.py:73
  40.2 1.2 sort.49
  41.5 19.8 %all-to-all-done.1 = bf16[8,2,128,256]{3,2,1,0:T(8,128)(2,1)S(1)} async-done(((bf16[8,2,128,256]{3,2,1,0:T(8,128)(2,1)}), bf16[8,2,128,256]{3,2,1,0:T(8,128)(2,1)S(1)}, u32[]{:S(2)}, u32[]{:S(2)}) %all-to-all-start.1) | async-done | bytes 1048608 | tf_op jit(solution)/shard_map/all_to_all | solution.py:32
  61.3 76.0 %all-gather.2.cloned.1.call-done = bf16[2048,1792]{0,1:T(8,128)(2,1)} async-done(((bf16[128,1792]{0,1:T(8,128)(2,1)}), bf16[2048,1792]{0,1:T(8,128)(2,1)}) %all-gather.2.cloned.1.call-update) | async-done | bytes 7340048 | tf_op jit(solution)/shard_map/all_gather | solution.py:63
  137.3 10.6 %fusion.1 = (bf16[256,1792]{0,1:T(8,128)(2,1)}, f32[256,1792]{0,1:T(8,128)}, f32[256,1792]{0,1:T(8,128)}, f32[256,1792]{0,1:T(8,128)S(1)}) fusion(f32[256,1792]{0,1:T(8,128)} %copy.60, f32[256,1792]{0,1:T(8,128)} %copy.52, f32[256,1792]{0,1:T(8,128)} %copy.58, bf16[2048,1792]{0,1:T(8,128)(2,1)} %all-gather.2.cloned.1.call-done, bf16[2048,256]{1,0:T(8,128)(2,1)} %bitcast.26), kind=kOutput, calls=%fused_computation.36 | convolution fusion | flops 1886388224 | bytes 20316160 | tf_op jit(solution)/shard_map/dot_general | solution.py:61
  147.9 1.8 gather_fusion.2
  149.7 1.1 select_bitcast_fusion
  150.8 4.3 %all-to-all-start.2 = ((bf16[256,16,112]{0,2,1:T(8,128)(2,1)}), bf16[256,16,112]{0,2,1:T(8,128)(2,1)S(1)}, u32[]{:S(2)}, u32[]{:S(2)}) async-start(bf16[256,16,112]{0,2,1:T(8,128)(2,1)} %select_bitcast_fusion), calls=%async_computation.2 | async-start | bytes 1835008 | tf_op jit(solution)/shard_map/all_to_all | solution.py:79
  155.1 3.2 %sort.50 = (s32[256]{0:T(256)}, s32[256]{0:T(256)S(1)}) sort(s32[256]{0:T(256)S(1)} %copy-done.5, s32[256]{0:T(256)S(1)} %iota.19), dimensions={0}, to_apply=%region_2.4 | sort | flops 2048 | bytes 4096 | tf_op jit(solution)/shard_map/jit(argsort)/sort | solution.py:74
  159.0 2.7 %copy.61 = f32[256,1792]{1,0:T(8,128)} copy(f32[256,1792]{0,1:T(8,128)} %get-tuple-element.34) | data formatting | bytes 3670016
  161.7 2.7 %copy.62 = f32[256,1792]{1,0:T(8,128)} copy(f32[256,1792]{0,1:T(8,128)} %get-tuple-element.35) | data formatting | bytes 3670016
  164.5 1.7 copy.63
  166.1 13.3 %all-to-all-done.2 = bf16[256,16,112]{0,2,1:T(8,128)(2,1)S(1)} async-done(((bf16[256,16,112]{0,2,1:T(8,128)(2,1)}), bf16[256,16,112]{0,2,1:T(8,128)(2,1)S(1)}, u32[]{:S(2)}, u32[]{:S(2)}) %all-to-all-start.2) | async-done | bytes 917536 | tf_op jit(solution)/shard_map/all_to_all | solution.py:79
  180.2 1.4 copy.64
  (32 shorter events, 3.4 us)
Async XLA Ops:
  7.2 4.4 %copy-start.2 = (bf16[1,128,4096]{2,1,0:T(8,128)(2,1)S(1)}, bf16[1,128,4096]{2,1,0:T(8,128)(2,1)}, u32[]{:S(2)}) copy-start(bf16[1,128,4096]{2,1,0:T(8,128)(2,1)} %param.12) | copy-start | bytes 3145732
  7.2 130.2 %all-gather.2.cloned.1.call-start = ((), (), s32[]{:S(2)}) async-start(), calls=%async_computation.3 | async-start | bytes 7798784 | tf_op jit(solution)/shard_map/all_gather | solution.py:63
  20.2 10.0 %copy-start = (f32[256,1792]{1,0:T(8,128)S(1)}, f32[256,1792]{1,0:T(8,128)}, u32[]{:S(2)}) copy-start(f32[256,1792]{1,0:T(8,128)} %param.18) | copy-start | bytes 5505028
  21.3 40.1 %all-to-all-start.1 = ((bf16[8,2,128,256]{3,2,1,0:T(8,128)(2,1)}), bf16[8,2,128,256]{3,2,1,0:T(8,128)(2,1)S(1)}, u32[]{:S(2)}, u32[]{:S(2)}) async-start(bf16[8,2,128,256]{3,2,1,0:T(8,128)(2,1)} %copy.57), calls=%async_computation.1 | async-start | bytes 2097152 | tf_op jit(solution)/shard_map/all_to_all | solution.py:32
  31.9 2.9 %copy-start.1 = (f32[256,1792]{1,0:T(8,128)S(1)}, f32[256,1792]{1,0:T(8,128)}, u32[]{:S(2)}) copy-start(f32[256,1792]{1,0:T(8,128)} %param.17) | copy-start | bytes 5505028
  34.7 1.7 copy-start.4
  61.3 76.0 %copy-start.3 = (bf16[8,2,128,256]{3,2,1,0:T(8,128)(2,1)}, bf16[8,2,128,256]{3,2,1,0:T(8,128)(2,1)S(1)}, u32[]{:S(2)}) copy-start(bf16[8,2,128,256]{3,2,1,0:T(8,128)(2,1)S(1)} %all-to-all-done.1) | copy-start | bytes 3145732
  149.7 5.4 %copy-start.5 = (s32[256]{0:T(256)S(1)}, s32[256]{0:T(256)}, u32[]{:S(2)}) copy-start(s32[256]{0:T(256)} %param.15) | copy-start | bytes 3076
  150.8 28.6 %all-to-all-start.2 = ((bf16[256,16,112]{0,2,1:T(8,128)(2,1)}), bf16[256,16,112]{0,2,1:T(8,128)(2,1)S(1)}, u32[]{:S(2)}, u32[]{:S(2)}) async-start(bf16[256,16,112]{0,2,1:T(8,128)(2,1)} %select_bitcast_fusion), calls=%async_computation.2 | async-start | bytes 1835008 | tf_op jit(solution)/shard_map/all_to_all | solution.py:79
Sparse Core Ops, SparseCore 0:
  11.7 125.5 all-gather.1
where the time goes:
time: 189 us; the launch traced here: 188 us
  waiting for transfers between devices  109 us (58%)
  local copies, waits for them, and re-layouts  22 us (12%)
  between operations  14.9 us (8%)
  starting transfers between devices  13.3 us (7%)
  other arithmetic  11.1 us (6%)
  matrix products  10.6 us (6%)
  blocking collectives  7.4 us (4%)
    all_gather x1, waiting for transfers between devices, on_device(): lax.all_gather(masked, DP, axis=0, tiled=True)  76 us
    all_to_all x1, waiting for transfers between devices, exchange_in_order(): out = lax.all_to_all(out, axes[k], k, k, tiled=True)  19.8 us
    unnamed x21, local copies, waits for them, and re-layouts  16.7 us
    all_to_all x1, waiting for transfers between devices, on_device(): lax.all_to_all(outgoing, 'expert', split_axis=1, concat_axis=1, tiled=True)  13.3 us
    dot_general x1, matrix products, on_device(): lax.dot_general(sliced, lax.all_gather(masked, DP, axis=0, tiled=True), c...  10.6 us
    all_to_all x1, starting transfers between devices, exchange_in_order(): out = lax.all_to_all(out, axes[k], k, k, tiled=True)  8.94 us
    all_to_all x1, blocking collectives, exchange_in_order(): out = lax.all_to_all(out, axes[k], k, k, tiled=True)  7.4 us
    all_to_all x1, starting transfers between devices, on_device(): lax.all_to_all(outgoing, 'expert', split_axis=1, concat_axis=1, tiled=True)  4.34 us
  transfers between devices with their start and end apart: 3, of which 3 were waited for; matrix products, arithmetic and copies ran while one was open for 13% of the time, Pallas kernels for 0%

commit v1 on v0

--- a/solution.py
+++ b/solution.py
@@ -12,6 +12,13 @@
 decay_rate = 0.1
 epsilon = 1e-08
 step_count = 100.0
+
+
+def gather_over(x, name, along):
+    devices = lax.axis_size(name)
+    blocks = jnp.stack([x for _ in range(devices)])
+    blocks = lax.all_to_all(blocks, name, split_axis=0, concat_axis=0)
+    return jnp.concatenate(blocks, axis=along)
 
 
 def split_up(value, dim, devices):
@@ -59,10 +66,7 @@
     contract = (((0,), (0,)), ((), ()))
     sliced = core_and_chips(outgrad, (("dp_0", "dp_1"), "dp_2"), (1, 0), 1, 0)
     gradient = lax.dot_general(
-        sliced,
-        lax.all_gather(masked, DP, axis=0, tiled=True),
-        contract,
-        preferred_element_type=jnp.float32,
+        sliced, gather_over(masked, DP, 0), contract, preferred_element_type=jnp.float32
     )
     new_moment1 = beta_one * moment1 + (1.0 - beta_one) * gradient
     new_moment2 = beta_two * moment2 + (1.0 - beta_two) * gradient * gradient

time: 189 us -> 270 us (1.43)
  starting transfers between devices: 13.3 us -> 106 us
  between operations: 14.9 us -> 1.43 us
  local copies, waits for them, and re-layouts: 22 us -> 25.9 us
    all_to_all x1, starting transfers between devices: 4.34 us -> 86.3 us  [on_device(): lax.all_to_all(outgoing, 'expert', split_axis=1, concat_axis=1, tiled=True)]
    all_gather x1 -> x0, waiting for transfers between devices: 76 us -> none  [on_device(): lax.all_gather(masked, DP, axis=0, tiled=True)]
    all_to_all x0 -> x1, waiting for transfers between devices: none -> 75.9 us  [gather_over(): blocks = lax.all_to_all(blocks, name, split_axis=0, concat_axis=0)]
    all_to_all x0 -> x1, starting transfers between devices: none -> 10.4 us  [gather_over(): blocks = lax.all_to_all(blocks, name, split_axis=0, concat_axis=0)]
    another operation x0 -> x2, local copies, waits for them, and re-layouts: none -> 3.96 us  [gather_over(): blocks = jnp.stack([x for _ in range(devices)])]
    unnamed x21 -> x23, local copies, waits for them, and re-layouts: 16.7 us -> 16.6 us
  transfers between devices with their start and end apart: 3 -> 3, of which waited for: 3 -> 3; matrix products, arithmetic and copies ran while one was open for 13% -> 9% of each run, Pallas kernels for 0% -> 0%
where the time goes in v1:
time: 270 us; the launch traced here: 269 us
  waiting for transfers between devices  109 us (40%)
  starting transfers between devices  106 us (39%)
  local copies, waits for them, and re-layouts  25.9 us (10%)
  matrix products  10.5 us (4%)
  other arithmetic  9.08 us (3%)
  blocking collectives  7.4 us (3%)
    all_to_all x1, starting transfers between devices, on_device(): lax.all_to_all(outgoing, 'expert', split_axis=1, concat_axis=1, tiled=True)  86.3 us
    all_to_all x1, waiting for transfers between devices, gather_over(): blocks = lax.all_to_all(blocks, name, split_axis=0, concat_axis=0)  75.9 us
    all_to_all x1, waiting for transfers between devices, exchange_in_order(): out = lax.all_to_all(out, axes[k], k, k, tiled=True)  20 us
    unnamed x23, local copies, waits for them, and re-layouts  16.6 us
    all_to_all x1, waiting for transfers between devices, on_device(): lax.all_to_all(outgoing, 'expert', split_axis=1, concat_axis=1, tiled=True)  13.2 us
    dot_general x1, matrix products, on_device(): lax.dot_general(sliced, gather_over(masked, DP, 0), contract, preferred_e...  10.5 us
    all_to_all x1, starting transfers between devices, gather_over(): blocks = lax.all_to_all(blocks, name, split_axis=0, concat_axis=0)  10.4 us
    all_to_all x1, starting transfers between devices, exchange_in_order(): out = lax.all_to_all(out, axes[k], k, k, tiled=True)  9.07 us
  transfers between devices with their start and end apart: 3, of which 3 were waited for; matrix products, arithmetic and copies ran while one was open for 9% of the time, Pallas kernels for 0%

profile of v1, /device:TPU:1, one launch (start us, length us, event | category | flops | bytes accessed | tf_op | source)
XLA Modules:
  0.0 269.2 jit_solution(223900592269281121)
XLA Ops:
  0.6 1.6 copy.58
  2.8 7.4 %all_to_all.21 = bf16[8,2,128,256]{3,2,0,1:T(8,128)(2,1)S(1)} all-to-all(bf16[8,2,128,256]{3,2,0,1:T(8,128)(2,1)S(1)} %copy.60), channel_id=1, replica_groups=mesh['dp_0'=4,'dp_1'=2,'dp_2'=2,'expert'=16] {'dp_2'}, dimensions={1} | all-to-all | bytes 2097152 | tf_op jit(solution)/shard_map/all_to_all | solution.py:39
  10.2 1.0 copy.61
  11.2 9.1 %all-to-all-start.2 = ((bf16[8,2,128,256]{3,2,1,0:T(8,128)(2,1)}), bf16[8,2,128,256]{3,2,1,0:T(8,128)(2,1)S(1)}, u32[]{:S(2)}, u32[]{:S(2)}) async-start(bf16[8,2,128,256]{3,2,1,0:T(8,128)(2,1)} %copy.61), calls=%async_computation.2 | async-start | bytes 2097152 | tf_op jit(solution)/shard_map/all_to_all | solution.py:39
  21.7 20.0 %all-to-all-done.2 = bf16[8,2,128,256]{3,2,1,0:T(8,128)(2,1)S(1)} async-done(((bf16[8,2,128,256]{3,2,1,0:T(8,128)(2,1)}), bf16[8,2,128,256]{3,2,1,0:T(8,128)(2,1)S(1)}, u32[]{:S(2)}, u32[]{:S(2)}) %all-to-all-start.2) | async-done | bytes 1048608 | tf_op jit(solution)/shard_map/all_to_all | solution.py:39
  41.7 3.7 %stack.5 = bf16[16,128,1792]{2,1,0:T(8,128)(2,1)} broadcast(bf16[128,1792]{1,0:T(8,128)(2,1)S(1)} %copy.57), dimensions={1,2} | broadcast | bytes 7798784 | tf_op jit(solution)/shard_map/stack | solution.py:19
  45.5 10.4 %all-to-all-start = ((bf16[16,128,1792]{2,1,0:T(8,128)(2,1)}), bf16[16,128,1792]{2,1,0:T(8,128)(2,1)}, u32[]{:S(2)}, u32[]{:S(2)}) async-start(bf16[16,128,1792]{2,1,0:T(8,128)(2,1)} %stack.5), calls=%async_computation | async-start | bytes 14680064 | tf_op jit(solution)/shard_map/all_to_all | solution.py:20
  55.9 1.7 copy.55
  57.6 2.9 %copy.62 = f32[256,1792]{0,1:T(8,128)} copy(f32[256,1792]{1,0:T(8,128)} %param.19) | data formatting | bytes 3670016 | tf_op args[8]
  60.4 1.7 copy.64
  62.1 3.2 %sort.48 = (s32[256]{0:T(256)}, s32[256]{0:T(256)S(1)}) sort(s32[256]{0:T(256)S(1)} %copy-done.4, s32[256]{0:T(256)S(1)} %iota.17), dimensions={0}, to_apply=%region_0.1 | sort | flops 2048 | bytes 4096 | tf_op jit(solution)/shard_map/jit(argsort)/sort | solution.py:77
  65.3 0.7 gather_fusion
  66.0 1.2 sort.49
  67.3 75.9 %all-to-all-done = bf16[16,128,1792]{2,1,0:T(8,128)(2,1)} async-done(((bf16[16,128,1792]{2,1,0:T(8,128)(2,1)}), bf16[16,128,1792]{2,1,0:T(8,128)(2,1)}, u32[]{:S(2)}, u32[]{:S(2)}) %all-to-all-start) | async-done | bytes 7340064 | tf_op jit(solution)/shard_map/all_to_all | solution.py:20
  143.1 10.5 %fusion.1 = (bf16[256,1792]{0,1:T(8,128)(2,1)}, f32[256,1792]{0,1:T(8,128)}, f32[256,1792]{0,1:T(8,128)}, f32[256,1792]{0,1:T(8,128)S(1)}) fusion(f32[256,1792]{0,1:T(8,128)} %copy.64, f32[256,1792]{0,1:T(8,128)} %copy.55, f32[256,1792]{0,1:T(8,128)} %copy.62, bf16[2048,1792]{1,0:T(8,128)(2,1)} %bitcast.4, bf16[2048,256]{1,0:T(8,128)(2,1)} %bitcast.27), kind=kOutput, calls=%fused_computation.36 | convolution fusion | flops 1886388224 | bytes 20316160 | tf_op jit(solution)/shard_map/dot_general | solution.py:68
  153.6 1.8 gather_fusion.2
  155.4 1.1 select_bitcast_fusion
  156.5 86.3 %all-to-all-start.3 = ((bf16[256,16,112]{0,2,1:T(8,128)(2,1)}), bf16[256,16,112]{0,2,1:T(8,128)(2,1)S(1)}, u32[]{:S(2)}, u32[]{:S(2)}) async-start(bf16[256,16,112]{0,2,1:T(8,128)(2,1)} %select_bitcast_fusion), calls=%async_computation.3 | async-start | bytes 1835008 | tf_op jit(solution)/shard_map/all_to_all | solution.py:83
  242.9 3.2 %sort.50 = (s32[256]{0:T(256)}, s32[256]{0:T(256)S(1)}) sort(s32[256]{0:T(256)S(1)} %copy-done.5, s32[256]{0:T(256)S(1)} %iota.19), dimensions={0}, to_apply=%region_2.4 | sort | flops 2048 | bytes 4096 | tf_op jit(solution)/shard_map/jit(argsort)/sort | solution.py:78
  246.7 2.7 %copy.65 = f32[256,1792]{1,0:T(8,128)} copy(f32[256,1792]{0,1:T(8,128)} %get-tuple-element.34) | data formatting | bytes 3670016
  249.5 2.7 %copy.66 = f32[256,1792]{1,0:T(8,128)} copy(f32[256,1792]{0,1:T(8,128)} %get-tuple-element.35) | data formatting | bytes 3670016
  252.2 1.7 copy.67
  253.9 13.2 %all-to-all-done.3 = bf16[256,16,112]{0,2,1:T(8,128)(2,1)S(1)} async-done(((bf16[256,16,112]{0,2,1:T(8,128)(2,1)}), bf16[256,16,112]{0,2,1:T(8,128)(2,1)S(1)}, u32[]{:S(2)}, u32[]{:S(2)}) %all-to-all-start.3) | async-done | bytes 917536 | tf_op jit(solution)/shard_map/all_to_all | solution.py:83
  267.9 1.4 copy.68
  (35 shorter events, 2.7 us)
Async XLA Ops:
  10.2 10.8 %copy-start.3 = (bf16[1,128,1792]{2,1,0:T(8,128)(2,1)S(1)}, bf16[1,128,1792]{2,1,0:T(8,128)(2,1)}, u32[]{:S(2)}) copy-start(bf16[1,128,1792]{2,1,0:T(8,128)(2,1)} %param.11) | copy-start | bytes 1376260
  11.2 10.0 %copy-start.4 = (s32[256]{0:T(256)S(1)}, s32[256]{0:T(256)}, u32[]{:S(2)}) copy-start(s32[256]{0:T(256)} %param.16) | copy-start | bytes 3076
  11.2 10.0 %copy-start.5 = (s32[256]{0:T(256)S(1)}, s32[256]{0:T(256)}, u32[]{:S(2)}) copy-start(s32[256]{0:T(256)} %param.15) | copy-start | bytes 3076
  11.2 10.1 %copy-start.6 = (s32[1,128]{1,0:T(1,128)S(1)}, s32[1,128]{1,0:T(1,128)}, u32[]{:S(2)}) copy-start(s32[1,128]{1,0:T(1,128)} %param.13) | copy-start | bytes 1540
  11.2 30.5 %all-to-all-start.2 = ((bf16[8,2,128,256]{3,2,1,0:T(8,128)(2,1)}), bf16[8,2,128,256]{3,2,1,0:T(8,128)(2,1)S(1)}, u32[]{:S(2)}, u32[]{:S(2)}) async-start(bf16[8,2,128,256]{3,2,1,0:T(8,128)(2,1)} %copy.61), calls=%async_computation.2 | async-start | bytes 2097152 | tf_op jit(solution)/shard_map/all_to_all | solution.py:39
  41.7 3.8 %copy-start.2 = (bf16[8,2,128,256]{3,2,1,0:T(8,128)(2,1)}, bf16[8,2,128,256]{3,2,1,0:T(8,128)(2,1)S(1)}, u32[]{:S(2)}) copy-start(bf16[8,2,128,256]{3,2,1,0:T(8,128)(2,1)S(1)} %all-to-all-done.2) | copy-start | bytes 3145732
  45.5 10.4 %copy-start = (f32[256,1792]{1,0:T(8,128)S(1)}, f32[256,1792]{1,0:T(8,128)}, u32[]{:S(2)}) copy-start(f32[256,1792]{1,0:T(8,128)} %param.18) | copy-start | bytes 5505028
  45.5 97.7 %all-to-all-start = ((bf16[16,128,1792]{2,1,0:T(8,128)(2,1)}), bf16[16,128,1792]{2,1,0:T(8,128)(2,1)}, u32[]{:S(2)}, u32[]{:S(2)}) async-start(bf16[16,128,1792]{2,1,0:T(8,128)(2,1)} %stack.5), calls=%async_computation | async-start | bytes 14680064 | tf_op jit(solution)/shard_map/all_to_all | solution.py:20
  57.6 2.9 %copy-start.1 = (f32[256,1792]{1,0:T(8,128)S(1)}, f32[256,1792]{1,0:T(8,128)}, u32[]{:S(2)}) copy-start(f32[256,1792]{1,0:T(8,128)} %param.17) | copy-start | bytes 5505028
  156.5 110.6 %all-to-all-start.3 = ((bf16[256,16,112]{0,2,1:T(8,128)(2,1)}), bf16[256,16,112]{0,2,1:T(8,128)(2,1)S(1)}, u32[]{:S(2)}, u32[]{:S(2)}) async-start(bf16[256,16,112]{0,2,1:T(8,128)(2,1)} %select_bitcast_fusion), calls=%async_computation.3 | async-start | bytes 1835008 | tf_op jit(solution)/shard_map/all_to_all | solution.py:83
